TPU v7x, 32 devices: a whole 2x2x4 slice. The times are simulated.
32 devices in a mesh: dp: 4 (over y, x), mp: 8 (over z, core).
Axes of the slice: x: 2, y: 2, z: 4, core: 2. Of those that a mesh axis runs over, the one named last changes fastest.
Arguments:
- tokens: bfloat16 [128, 6144], P(('dp', 'mp')), may hold values from -6 to 6
- norm_gain: float32 [6144], replicated, may hold values from 0.5 to 1.5
- w_query: bfloat16 [6144, 4096], P('dp', 'mp'), as said below
- w_key: bfloat16 [6144, 4096], P('dp', 'mp'), as said below
- w_value: bfloat16 [6144, 4096], P('dp', 'mp'), may hold values from -0.078125 to 0.078125
- w_inner: bfloat16 [6144, 24576], P('dp', 'mp'), may hold values from -0.078125 to 0.078125
- bias_inner: float32 [24576], P('mp'), may hold values from -3 to 3
- w_attn_out: bfloat16 [4096, 6144], P('mp', 'dp'), may hold values from -0.09375 to 0.09375
- w_outer: bfloat16 [24576, 6144], P('mp', 'dp'), may hold values from -0.0390625 to 0.0390625
- temper: float32 [32], P('mp'), may hold values from 0.5 to 24
Outputs:
- result: bfloat16 [128, 6144], P(('dp', 'mp'))
Inputs may be any that keep to these rules, and one draw needn't show every extreme that they name: `w_query`: entries of order 6144 ** -0.5. `w_key`: entries of order 6144 ** -0.5.
All inputs are finite; a program needn't handle non-finite values.
Results may differ from a plain program's by a relative error of at most 0.023.
Values may be sent and summed in bfloat16 or wider, within the bound.
A program may use at most 128 MiB of HBM per device.

v0:
```python
import functools
import math

import jax
import jax.numpy as jnp
from jax import lax
from jax.experimental import pallas as pl
from jax.experimental.pallas import tpu as pltpu
from jax.sharding import PartitionSpec as P

HEAD = 128
LAG_SUM = 5
LAG_PASS = 7
MESH = pl.DeviceIdType.MESH
F32, BF16 = jnp.float32, jnp.bfloat16


def normalize(values):
    center = values - jnp.mean(values, axis=-1, keepdims=True)
    spread = jnp.mean(center * center, axis=-1, keepdims=True)
    return center * lax.rsqrt(spread + 1e-06)


def wait_bytes(ref, sem):
    pltpu.make_async_copy(ref, ref, sem).wait()


def block_kernel(
    n_dp, n_mp,
    tokens, gain, bias, temper, w_query, w_key, w_value, w_inner, w_attn, w_outer,
    out,
    w_in, w_out, nsend, nrecv, stage, x, psend, precv, ag, acc, xsend, xrecv, dsend, drecv,
    win_sem, wout_sem, a_send, a_recv, f_send, f_recv, p_send, p_recv, g_send, g_recv,
    x_send, x_recv, d_send, d_recv,
):
    n_dev = n_dp * n_mp
    rows = tokens.shape[0]
    n_in, depth, wide = w_in.shape
    n_out = w_out.shape[0]
    per = psend.shape[2]
    i, j = lax.axis_index("dp"), lax.axis_index("mp")
    me = i * n_mp + j
    n_chip = n_mp // 2
    n_lane = n_dp * n_chip
    core, chip = lax.rem(j, 2), j // 2
    sibling = (i, j + 1 - 2 * core)
    lane = i * n_chip + chip

    def same_core(other):
        return (other // n_chip, 2 * lax.rem(other, n_chip) + core)

    barrier = pltpu.get_barrier_semaphore()

    def greet(d, carry):
        t = lax.rem(me + d, n_dev)
        pl.semaphore_signal(
            barrier, inc=1, device_id=(t // n_mp, lax.rem(t, n_mp)), device_id_type=MESH
        )
        return carry

    lax.fori_loop(1, n_dev, greet, 0)

    for c, w in enumerate((w_query, w_key, w_value)):
        pltpu.make_async_copy(w, w_in.at[c], win_sem.at[c]).start()
    for c in range(3, n_in):
        pltpu.make_async_copy(
            w_inner.at[:, pl.ds((c - 3) * wide, wide)], w_in.at[c], win_sem.at[c]
        ).start()
    pltpu.make_async_copy(w_attn, w_out.at[0], wout_sem.at[0]).start()
    for c in range(1, n_out):
        pltpu.make_async_copy(
            w_outer.at[pl.ds((c - 1) * wide, wide), :], w_out.at[c], wout_sem.at[c]
        ).start()

    normed = (normalize(tokens[...].astype(F32)) * gain[...]).astype(BF16)
    for p in range(n_dp):
        nsend[p] = normed[:, p * depth : (p + 1) * depth]
    nrecv[me] = nsend[i]
    pl.semaphore_wait(barrier, n_dev - 1)

    def scatter_normed(d, carry):
        target = same_core(lax.rem(lane + d, n_lane))
        pltpu.make_async_remote_copy(
            src_ref=nsend.at[target[0]], dst_ref=nrecv.at[me],
            send_sem=a_send, recv_sem=a_recv.at[d],
            device_id=target, device_id_type=MESH,
        ).start()
        return carry

    def pass_on(source):
        pltpu.make_async_remote_copy(
            src_ref=nrecv.at[source], dst_ref=nrecv.at[source], send_sem=f_send, recv_sem=f_recv,
            device_id=sibling, device_id_type=MESH,
        ).start()

    lax.fori_loop(1, n_lane, scatter_normed, 0)
    pass_on(me)

    def forward_normed(d, carry):
        wait_bytes(nrecv.at[0], a_recv.at[d])
        source = same_core(lax.rem(lane + n_lane - d, n_lane))
        pass_on(source[0] * n_mp + source[1])
        return carry

    lax.fori_loop(1, n_lane, forward_normed, 0)
    wait_bytes(nrecv.at[pl.ds(0, n_lane)], f_recv)
    for s in range(n_dev):
        stage[s * rows : (s + 1) * rows, :] = nrecv[s].astype(F32)
    x[...] = stage[...].astype(BF16)

    square = n_dp == 4

    def around(c):
        beside = i + 1 - 2 * lax.rem(i, 2)
        across = lax.rem(i + 2, n_dp)
        turn = lax.rem(c, 2)
        return beside + turn * (across - beside), across + turn * (beside - across)

    def send(source, target, send_sem, recv_sem, p):
        pltpu.make_async_remote_copy(
            src_ref=source, dst_ref=target, send_sem=send_sem, recv_sem=recv_sem,
            device_id=(p, j), device_id_type=MESH,
        ).start()

    def project(c, carry):
        pltpu.make_async_copy(w_query, w_in.at[c], win_sem.at[c]).wait()
        part = jnp.dot(x[...], w_in[c], preferred_element_type=F32).astype(BF16)
        psend[c] = part.reshape(n_dp, per, wide)
        if square:
            first, _ = around(c)
            send(psend.at[c, 3 - i], precv.at[c, 1], p_send, p_recv.at[c, 1], first)
            send(psend.at[c, first], precv.at[c, 0], p_send, p_recv.at[c, 0], first)
            pl.when(c >= LAG_SUM)(lambda: add_and_send(c - LAG_SUM))
        else:
            precv[c, i] = psend[c, i]
            for d in range(1, n_dp):
                p = lax.rem(i + d, n_dp)
                send(psend.at[c, p], precv.at[c, i], p_send, p_recv.at[c, 0], p)
        return carry

    def add_and_send(c):
        _, second = around(c)
        wait_bytes(precv.at[c, 1], p_recv.at[c, 1])
        precv[c, 3] = (psend[c, second].astype(F32) + precv[c, 1].astype(F32)).astype(BF16)
        send(precv.at[c, 3], precv.at[c, 2], p_send, p_recv.at[c, 2], second)

    lax.fori_loop(0, n_in, project, 0)
    if square:
        for c in range(max(n_in - LAG_SUM, 0), n_in):
            add_and_send(c)

    def reduced(c):
        if square:
            wait_bytes(precv.at[c, 0], p_recv.at[c, 0])
            wait_bytes(precv.at[c, 2], p_recv.at[c, 2])
            total = psend[c, i].astype(F32) + precv[c, 0].astype(F32)
            return total + precv[c, 2].astype(F32)
        wait_bytes(precv.at[c, pl.ds(0, n_dp - 1)], p_recv.at[c, 0])
        total = precv[c, 0].astype(F32)
        for p in range(1, n_dp):
            total = total + precv[c, p].astype(F32)
        return total

    def share(h, value):
        ag[h, i] = value
        own = ag.at[h, i]
        if square:
            first, second = around(h)
            send(own, own, g_send, g_recv.at[h, 0], second)
            send(own, own, g_send, g_recv.at[h, 1], first)
        else:
            for d in range(1, n_dp):
                send(own, own, g_send, g_recv.at[h, 0], lax.rem(i + d, n_dp))

    def hand_over(h):
        first, second = around(h)
        block = ag.at[h, second]
        wait_bytes(block, g_recv.at[h, 0])
        send(block, block, g_send, g_recv.at[h, 2], first)

    query, key, value = reduced(0), reduced(1), reduced(2)
    mixed = []
    for h in range(wide // HEAD):
        cols = slice(h * HEAD, (h + 1) * HEAD)
        query_norm = normalize(query[:, cols].astype(BF16).astype(F32)).astype(BF16)
        key_norm = normalize(key[:, cols].astype(BF16).astype(F32)).astype(BF16)
        scores = lax.dot_general(
            query_norm, key_norm, (((1,), (1,)), ((), ())), preferred_element_type=F32
        )
        scores = scores * (temper[h] * (1.0 / math.sqrt(HEAD)))
        weight = jnp.exp(scores - jnp.max(scores, axis=-1, keepdims=True))
        probs = (weight / jnp.sum(weight, axis=-1, keepdims=True)).astype(BF16)
        mixed.append(
            jnp.dot(probs, value[:, cols].astype(BF16), preferred_element_type=F32).astype(BF16)
        )
    share(0, jnp.concatenate(mixed, axis=1))

    def activate(h, carry):
        at = pl.multiple_of((h - 1) * wide, HEAD)
        inner = reduced(h + 2) + bias[:, pl.ds(at, wide)]
        activ = 0.5 * inner * (1.0 + lax.erf(inner * math.sqrt(0.5)))
        share(h, activ.astype(BF16))
        if square:
            pl.when(h >= LAG_PASS)(lambda: hand_over(h - LAG_PASS))
        return carry

    lax.fori_loop(1, n_out, activate, 0)
    if square:
        for h in range(max(n_out - LAG_PASS, 0), n_out):
            hand_over(h)

    acc[...] = jnp.zeros_like(acc)

    def project_out(h, carry):
        pltpu.make_async_copy(w_attn, w_out.at[h], wout_sem.at[h]).wait()
        if square:
            wait_bytes(ag.at[h, 0], g_recv.at[h, 1])
            wait_bytes(ag.at[h, 0], g_recv.at[h, 2])
        else:
            wait_bytes(ag.at[h, pl.ds(0, n_dp - 1)], g_recv.at[h, 0])
        acc[...] += jnp.dot(
            ag[h].reshape(n_dp * per, wide), w_out[h], preferred_element_type=F32
        ).reshape(acc.shape)
        return carry

    lax.fori_loop(0, n_out, project_out, 0)

    def halves(p, q):
        tile = acc[p, 2 * rows * q : 2 * rows * (q + 1), :]
        low, high = tile[:rows], tile[rows:]
        return jnp.where(core == 0, low, high), jnp.where(core == 0, high, low)

    for k in range(n_dp):
        p = lax.rem(i + 1 + k, n_dp)
        for q in range(n_chip):
            xsend[p, q] = halves(p, q)[1].astype(BF16)
        pltpu.make_async_remote_copy(
            src_ref=xsend.at[p], dst_ref=xrecv.at[p], send_sem=x_send, recv_sem=x_recv.at[k],
            device_id=sibling, device_id_type=MESH,
        ).start()

    for k in range(n_dp):
        p = lax.rem(i + 1 + k, n_dp)
        wait_bytes(xrecv.at[p], x_recv.at[k])
        for q in range(n_chip):
            dsend[p, q] = (halves(p, q)[0] + xrecv[p, q].astype(F32)).astype(BF16)

        def scatter_out(d, carry):
            q = lax.rem(chip + d, n_chip)
            pltpu.make_async_remote_copy(
                src_ref=dsend.at[p, q], dst_ref=drecv.at[lane], send_sem=d_send, recv_sem=d_recv,
                device_id=(p, 2 * q + core), device_id_type=MESH,
            ).start()
            return carry

        lax.fori_loop(1, n_chip if k == n_dp - 1 else n_chip + 1, scatter_out, 0)
    drecv[lane] = dsend[i, chip]
    wait_bytes(drecv.at[pl.ds(0, n_lane - 1)], d_recv)
    for p in range(n_dp):
        total = drecv[p * n_chip].astype(F32)
        for q in range(1, n_chip):
            total = total + drecv[p * n_chip + q].astype(F32)
        cols = slice(p * depth, (p + 1) * depth)
        out[:, cols] = (tokens[:, cols].astype(F32) + total).astype(BF16)

    wait_bytes(nrecv.at[pl.ds(0, n_lane - 1)], a_send)
    wait_bytes(nrecv.at[pl.ds(0, n_lane)], f_send)
    wait_bytes(precv.at[:, pl.ds(0, n_dp - 1)], p_send)
    wait_bytes(ag.at[:, pl.ds(0, n_dp - 1)], g_send)
    wait_bytes(xrecv, x_send)
    wait_bytes(drecv.at[pl.ds(0, n_lane - 1)], d_send)


def per_device(
    n_dp, n_mp,
    tokens, norm_gain, w_query, w_key, w_value, w_inner, bias_inner, w_attn_out, w_outer, temper
):
    rows, width = tokens.shape
    depth, wide = w_query.shape
    hidden = w_inner.shape[1]
    n_dev, per = n_dp * n_mp, n_mp * rows
    n_in, n_out = 3 + hidden // wide, 1 + hidden // wide
    vmem = pl.BlockSpec(memory_space=pltpu.VMEM)
    smem = pl.BlockSpec(memory_space=pltpu.SMEM)
    hbm = pl.BlockSpec(memory_space=pl.ANY)
    dma = pltpu.SemaphoreType.DMA
    return pl.pallas_call(
        functools.partial(block_kernel, n_dp, n_mp),
        out_shape=jax.ShapeDtypeStruct((rows, width), BF16),
        in_specs=[vmem, vmem, vmem, smem] + [hbm] * 6,
        out_specs=vmem,
        scratch_shapes=[
            pltpu.VMEM((n_in, depth, wide), BF16),
            pltpu.VMEM((n_out, wide, depth), BF16),
            pltpu.VMEM((n_dp, rows, depth), BF16),
            pltpu.VMEM((n_dev, rows, depth), BF16),
            pltpu.VMEM((n_dev * rows, depth), F32),
            pltpu.VMEM((n_dev * rows, depth), BF16),
            pltpu.VMEM((n_in, n_dp, per, wide), BF16),
            pltpu.VMEM((n_in, n_dp, per, wide), BF16),
            pltpu.VMEM((n_out, n_dp, per, wide), BF16),
            pltpu.VMEM((n_dp, per, depth), F32),
            pltpu.VMEM((n_dp, n_mp // 2, rows, depth), BF16),
            pltpu.VMEM((n_dp, n_mp // 2, rows, depth), BF16),
            pltpu.VMEM((n_dp, n_mp // 2, rows, depth), BF16),
            pltpu.VMEM((n_dev // 2, rows, depth), BF16),
            dma((n_in,)), dma((n_out,)), dma, dma((n_dev // 2,)), dma, dma, dma, dma((n_in, 3)),
            dma, dma((n_out, 3)), dma, dma((n_dp,)), dma, dma,
        ],
        compiler_params=pltpu.CompilerParams(
            collective_id=0, has_side_effects=True, vmem_limit_bytes=60 * 1024 * 1024
        ),
        name="encoder_block",
    )(
        tokens, norm_gain.reshape(1, -1), bias_inner.reshape(1, -1), temper,
        w_query, w_key, w_value, w_inner, w_attn_out, w_outer,
    )


def solution(mesh):
    return jax.shard_map(
        functools.partial(per_device, mesh.shape["dp"], mesh.shape["mp"]),
        mesh=mesh,
        in_specs=(
            P(("dp", "mp"), None),
            P(),
            P("dp", "mp"),
            P("dp", "mp"),
            P("dp", "mp"),
            P("dp", "mp"),
            P("mp"),
            P("mp", "dp"),
            P("mp", "dp"),
            P("mp"),
        ),
        out_specs=P(("dp", "mp"), None),
        check_vma=False,
    )
```

profile of v0, /device:TPU:0, one launch (start us, length us, event | category | flops | bytes accessed | tf_op | source)
XLA Modules:
  0.0 46.8 jit_solution(9344308323614493907)
XLA Ops:
  0.0 45.4 %encoder_block.1 = bf16[4,6144]{1,0:T(4,128)(2,1)} custom-call(bf16[4,6144]{1,0:T(4,128)(2,1)} %tokens.1, f32[1,6144]{1,0:T(1,128)} %bitcast.2, f32[1,3072]{1,0:T(1,128)} %bitcast.3, f32[4]{0:T(128)} %temper.1, bf16[1536,512]{1,0:T(8,128)(2,1)} %w_query.1, bf16[1536,512]{1,0:T(8,128)(2,1)} %w_key.1, bf16[1536,512]{1,0:T(8,128)(2,1)} %w_value.1, ...), custom_call_target="tpu_custom_call" | custom-call | tf_op jit(solution)/shard_map/encoder_block/pallas_call | solution.py:287
  45.4 1.4 %copy.12 = bf16[4,6144]{1,0:T(4,128)(2,1)} copy(bf16[4,6144]{1,0:T(4,128)(2,1)} %encoder_block.1) | data formatting | bytes 98304
where the time goes:
time: 47 us; the launch traced here: 46.8 us
  Pallas kernels  45.4 us (97%)
  local copies, waits for them, and re-layouts  1.44 us (3%)
    pallas_call x1, Pallas kernels, per_device(): pl.pallas_call(functools.partial(block_kernel, n_dp, n_mp), out_shape=jax...  45.4 us
    unnamed x1, local copies, waits for them, and re-layouts  1.44 us

commit v1 on v0

v1 whole, which is shorter than its diff:
```python
import functools
import math

import jax
import jax.numpy as jnp
from jax import lax
from jax.experimental import pallas as pl
from jax.experimental.pallas import tpu as pltpu
from jax.sharding import PartitionSpec as P

HEAD = 128
GROUP = 3
DIRECT_IN = ()
DIRECT_OUT = ()
MESH = pl.DeviceIdType.MESH
F32, BF16 = jnp.float32, jnp.bfloat16


def normalize(values):
    center = values - jnp.mean(values, axis=-1, keepdims=True)
    spread = jnp.mean(center * center, axis=-1, keepdims=True)
    return center * lax.rsqrt(spread + 1e-06)


def wait_bytes(ref, sem):
    pltpu.make_async_copy(ref, ref, sem).wait()


def block_kernel(
    n_dp, n_mp,
    tokens, gain, bias, temper, w_query, w_key, w_value, w_inner, w_attn, w_outer,
    out,
    tok, gain_v, bias_v, w_in, w_out, nsend, nrecv, stage, x, psend, precv, ag, acc,
    xsend, xrecv, dsend, drecv,
    in_sem, win_sem, wout_sem, a_send, a_recv, f_send, f_recv, p_send, p_recv, g_send, g_recv,
    x_send, x_recv, d_send, d_recv,
):
    rows = tok.shape[0]
    n_in, depth, wide = w_in.shape
    n_out = w_out.shape[0]
    per = psend.shape[2]
    i, j = lax.axis_index("dp"), lax.axis_index("mp")
    me = i * n_mp + j
    n_chip = n_mp // 2
    n_lane = n_dp * n_chip
    core, chip = lax.rem(j, 2), j // 2
    sibling = (i, j + 1 - 2 * core)
    lane = i * n_chip + chip
    square = n_dp == 4
    n_half = n_chip // 2
    spot = lax.rem(chip, n_half)
    halves = (chip // n_half, 1 - chip // n_half)

    inputs = [
        pltpu.make_async_copy(tokens, tok, in_sem.at[0]),
        pltpu.make_async_copy(gain, gain_v, in_sem.at[1]),
        pltpu.make_async_copy(bias, bias_v, in_sem.at[2]),
    ]
    for copy in inputs:
        copy.start()

    barrier = pltpu.get_barrier_semaphore()
    columns = [lax.rem(i + a, n_dp) for a in range(n_dp)]
    chips = [lax.rem(chip + b, n_chip) for b in range(n_chip)]
    for a in range(n_dp):
        for b in range(n_chip):
            if a or b:
                pl.semaphore_signal(
                    barrier, inc=1, device_id=(columns[a], 2 * chips[b] + core),
                    device_id_type=MESH,
                )
    pl.semaphore_signal(barrier, inc=1, device_id=sibling, device_id_type=MESH)

    for copy in inputs:
        copy.wait()
    for c, w in enumerate((w_query, w_key, w_value)):
        pltpu.make_async_copy(w, w_in.at[c], win_sem.at[0]).start()
    for c in range(3, n_in):
        pltpu.make_async_copy(
            w_inner.at[:, pl.ds((c - 3) * wide, wide)], w_in.at[c], win_sem.at[c // GROUP]
        ).start()
    pltpu.make_async_copy(w_attn, w_out.at[0], wout_sem.at[0]).start()
    for c in range(1, n_out):
        pltpu.make_async_copy(
            w_outer.at[pl.ds((c - 1) * wide, wide), :], w_out.at[c],
            wout_sem.at[(c - 1) // GROUP + 1],
        ).start()

    normed = (normalize(tok[...].astype(F32)) * gain_v[...]).astype(BF16)
    for p in range(n_dp):
        nsend[p] = normed[:, p * depth : (p + 1) * depth]
    nrecv[me] = nsend[i]
    pl.semaphore_wait(barrier, n_lane)

    def pass_on(source):
        pltpu.make_async_remote_copy(
            src_ref=nrecv.at[source], dst_ref=nrecv.at[source], send_sem=f_send, recv_sem=f_recv,
            device_id=sibling, device_id_type=MESH,
        ).start()

    for b in range(n_chip):
        for a in range(n_dp):
            if a or b:
                pltpu.make_async_remote_copy(
                    src_ref=nsend.at[columns[a]], dst_ref=nrecv.at[me],
                    send_sem=a_send, recv_sem=a_recv.at[b * n_dp + a],
                    device_id=(columns[a], 2 * chips[b] + core), device_id_type=MESH,
                ).start()
    pass_on(me)

    def forward(d, carry):
        wait_bytes(nrecv.at[0], a_recv.at[d])
        p = lax.rem(i + n_dp - lax.rem(d, n_dp), n_dp)
        q = lax.rem(chip + n_chip - d // n_dp, n_chip)
        pass_on(p * n_mp + 2 * q + core)
        return carry

    lax.fori_loop(1, n_lane, forward, 0)
    wait_bytes(nrecv.at[pl.ds(0, n_lane)], f_recv)
    for s in range(n_dp * n_mp):
        stage[s * rows : (s + 1) * rows, :] = nrecv[s].astype(F32)
    x[...] = stage[...].astype(BF16)

    def around(t):
        beside = i + 1 - 2 * lax.rem(i, 2)
        across = lax.rem(i + 2, n_dp)
        turn = lax.rem(t + core, 2)
        return beside + turn * (across - beside), across + turn * (beside - across)

    def send(source, target, send_sem, recv_sem, p):
        pltpu.make_async_remote_copy(
            src_ref=source, dst_ref=target, send_sem=send_sem, recv_sem=recv_sem,
            device_id=(p, j), device_id_type=MESH,
        ).start()

    def project(first, count):
        for r in range(count):
            c = first + r
            if c % GROUP == 0:
                wait_bytes(w_in.at[pl.ds(c, GROUP)], win_sem.at[c // GROUP])
        for r in range(count):
            c = first + r
            part = jnp.dot(x[...], w_in[c], preferred_element_type=F32).astype(BF16)
            psend[c] = part.reshape(n_dp, per, wide)
        for r in range(count):
            c = first + r
            if square and c not in DIRECT_IN:
                nearby, _ = around(c)
                send(psend.at[c, 3 - i], precv.at[c, 1], p_send, p_recv.at[c, 1], nearby)
                send(psend.at[c, nearby], precv.at[c, 0], p_send, p_recv.at[c, 0], nearby)
            else:
                precv[c, i] = psend[c, i]
                for d in range(1, n_dp):
                    p = lax.rem(i + d, n_dp)
                    send(psend.at[c, p], precv.at[c, i], p_send, p_recv.at[c, 0], p)

    def add_and_send(c):
        if not square or c in DIRECT_IN:
            return
        _, second = around(c)
        wait_bytes(precv.at[c, 1], p_recv.at[c, 1])
        precv[c, 3] = (psend[c, second].astype(F32) + precv[c, 1].astype(F32)).astype(BF16)
        send(precv.at[c, 3], precv.at[c, 2], p_send, p_recv.at[c, 2], second)

    def reduced(c):
        if square and c not in DIRECT_IN:
            wait_bytes(precv.at[c, 0], p_recv.at[c, 0])
            wait_bytes(precv.at[c, 2], p_recv.at[c, 2])
            total = psend[c, i].astype(F32) + precv[c, 0].astype(F32)
            return total + precv[c, 2].astype(F32)
        wait_bytes(precv.at[c, pl.ds(0, n_dp - 1)], p_recv.at[c, 0])
        total = precv[c, 0].astype(F32)
        for p in range(1, n_dp):
            total = total + precv[c, p].astype(F32)
        return total

    def hold(h, value):
        for half in range(2):
            ag[h, half, i] = value[half * (per // 2) : (half + 1) * (per // 2)]

    def block_of(h, half, p):
        return ag.at[h, :, p] if half is None else ag.at[h, halves[half], p]

    def lamp(h, half, step):
        return g_recv.at[h * 6 + 3 * (half or 0) + step]

    def share(h, half=None):
        own = block_of(h, half, i)
        if square and h not in DIRECT_OUT:
            first, second = around(h)
            send(own, own, g_send, lamp(h, half, 0), second)
            send(own, own, g_send, lamp(h, half, 1), first)
        else:
            for d in range(1, n_dp):
                send(own, own, g_send, lamp(h, half, 0), columns[d])

    def hand_over(h, half=None):
        if not square or h in DIRECT_OUT:
            return
        first, second = around(h)
        block = block_of(h, half, second)
        wait_bytes(block, lamp(h, half, 0))
        send(block, block, g_send, lamp(h, half, 2), first)

    def attend():
        query, key, value = (reduced(c).astype(BF16) for c in range(3))
        heads = range(wide // HEAD)
        cols = [slice(h * HEAD, (h + 1) * HEAD) for h in heads]
        tall = [t[:, cols[h]].astype(F32) for t in (query, key) for h in heads]
        tall = normalize(jnp.concatenate(tall, axis=0)).astype(BF16)
        pairs = [
            (tall[h * per : (h + 1) * per], tall[(len(heads) + h) * per : (len(heads) + h + 1) * per])
            for h in heads
        ]
        scores = jnp.concatenate([
            lax.dot_general(q, k, (((1,), (1,)), ((), ())), preferred_element_type=F32)
            * (temper[h] * (1.0 / math.sqrt(HEAD)))
            for h, (q, k) in zip(heads, pairs)
        ], axis=0)
        weight = jnp.exp(scores - jnp.max(scores, axis=-1, keepdims=True))
        probs = (weight / jnp.sum(weight, axis=-1, keepdims=True)).astype(BF16)
        mixed = [
            jnp.dot(
                probs[h * per : (h + 1) * per], value[:, cols[h]], preferred_element_type=F32
            ).astype(BF16)
            for h in heads
        ]
        hold(0, jnp.concatenate(mixed, axis=1))
        share(0)

    def activate(h, whole=True):
        at = (h - 1) * wide
        inner = reduced(h + 2) + bias_v[:, at : at + wide]
        activ = 0.5 * inner * (1.0 + lax.erf(inner * math.sqrt(0.5)))
        hold(h, activ.astype(BF16))
        if whole:
            share(h)

    def fetched(h, half=None):
        if half in (None, 1) and (h < 2 or (h - 1) % GROUP == 0):
            g = (h + GROUP - 1) // GROUP
            wait_bytes(w_out.at[pl.ds(0, min(h, 1) * (GROUP - 1) + 1)], wout_sem.at[g])
        block = block_of(h, half, 0)
        if square and h not in DIRECT_OUT:
            wait_bytes(block, lamp(h, half, 1))
            wait_bytes(block, lamp(h, half, 2))
        else:
            for d in range(1, n_dp):
                wait_bytes(block, lamp(h, half, 0))

    def project_out(hs, opened, half=None):
        for h in hs:
            fetched(h, half)
        total = None
        if opened:
            total = (acc[...] if half is None else acc[halves[half]]).reshape(-1, depth)
        for h in hs:
            left = (ag[h] if half is None else ag[h, halves[half]]).reshape(-1, wide)
            product = jnp.dot(left, w_out[h], preferred_element_type=F32)
            total = product if total is None else total + product
        if half is None:
            acc[...] = total.reshape(acc.shape)
        else:
            acc[halves[half]] = total.reshape(acc.shape[1:])

    def sorted_rows(half, p, q):
        tile = acc[halves[half], p, 2 * rows * q : 2 * rows * (q + 1), :]
        low, high = tile[:rows], tile[rows:]
        return jnp.where(core == 0, low, high), jnp.where(core == 0, high, low)

    def swap(half):
        for k in range(n_dp):
            p = columns[(k + 1) % n_dp]
            for q in range(n_half):
                xsend[half, p, q] = sorted_rows(half, p, q)[1].astype(BF16)
            pltpu.make_async_remote_copy(
                src_ref=xsend.at[half, p], dst_ref=xrecv.at[half, p],
                send_sem=x_send, recv_sem=x_recv.at[half, k],
                device_id=sibling, device_id_type=MESH,
            ).start()

    def deliver(half):
        for k in range(n_dp):
            p = columns[(k + 1) % n_dp]
            wait_bytes(xrecv.at[half, p], x_recv.at[half, k])
            for q in range(n_half):
                dsend[half, p, q] = (
                    sorted_rows(half, p, q)[0] + xrecv[half, p, q].astype(F32)
                ).astype(BF16)
            for b in list(range(1, n_half)) + [0]:
                if half or b or k < n_dp - 1:
                    q = lax.rem(spot + b, n_half)
                    pltpu.make_async_remote_copy(
                        src_ref=dsend.at[half, p, q], dst_ref=drecv.at[lane],
                        send_sem=d_send, recv_sem=d_recv,
                        device_id=(p, 2 * (halves[half] * n_half + q) + core),
                        device_id_type=MESH,
                    ).start()
        if not half:
            drecv[lane] = dsend[0, i, spot]

    project(0, 3)
    project(3, 3)
    for c in range(0, 3):
        add_and_send(c)
    project(6, 3)
    for c in range(3, 6):
        add_and_send(c)
    attend()
    for c in range(6, 9):
        add_and_send(c)
    for h in range(1, 4):
        activate(h)
    for h in range(0, 1):
        hand_over(h)
    for h in range(4, 7):
        activate(h)
    for h in range(1, 4):
        hand_over(h)
    project_out((0,), False)
    for h in range(4, 7):
        hand_over(h)
    project_out((1, 2), True)
    project_out((3,), True)
    project_out((4,), True)
    project_out((5,), True)
    project_out((6,), True)
    swap(1)
    deliver(1)
    swap(0)
    deliver(0)
    wait_bytes(drecv.at[pl.ds(0, n_lane - 1)], d_recv)
    for p in range(n_dp):
        total = drecv[p * n_chip].astype(F32)
        for q in range(1, n_chip):
            total = total + drecv[p * n_chip + q].astype(F32)
        cols = slice(p * depth, (p + 1) * depth)
        out[:, cols] = (tok[:, cols].astype(F32) + total).astype(BF16)

    wait_bytes(nrecv.at[pl.ds(0, n_lane - 1)], a_send)
    wait_bytes(nrecv.at[pl.ds(0, n_lane)], f_send)
    wait_bytes(precv.at[:, pl.ds(0, n_dp - 1)], p_send)
    wait_bytes(ag.at[:, :, pl.ds(0, n_dp - 1)], g_send)
    wait_bytes(xrecv, x_send)
    wait_bytes(drecv.at[pl.ds(0, n_lane - 1)], d_send)


def per_device(
    n_dp, n_mp,
    tokens, norm_gain, w_query, w_key, w_value, w_inner, bias_inner, w_attn_out, w_outer, temper
):
    rows, width = tokens.shape
    depth, wide = w_query.shape
    hidden = w_inner.shape[1]
    n_dev, per = n_dp * n_mp, n_mp * rows
    n_in, n_out = 3 + hidden // wide, 1 + hidden // wide
    vmem = pl.BlockSpec(memory_space=pltpu.VMEM)
    smem = pl.BlockSpec(memory_space=pltpu.SMEM)
    hbm = pl.BlockSpec(memory_space=pl.ANY)
    dma = pltpu.SemaphoreType.DMA
    return pl.pallas_call(
        functools.partial(block_kernel, n_dp, n_mp),
        out_shape=pltpu.VMEM((rows, width), BF16),
        in_specs=[hbm, hbm, hbm, smem] + [hbm] * 6,
        out_specs=vmem,
        scratch_shapes=[
            pltpu.VMEM((rows, width), BF16),
            pltpu.VMEM((1, width), F32),
            pltpu.VMEM((1, hidden), F32),
            pltpu.VMEM((n_in, depth, wide), BF16),
            pltpu.VMEM((n_out, wide, depth), BF16),
            pltpu.VMEM((n_dp, rows, depth), BF16),
            pltpu.VMEM((n_dev, rows, depth), BF16),
            pltpu.VMEM((n_dev * rows, depth), F32),
            pltpu.VMEM((n_dev * rows, depth), BF16),
            pltpu.VMEM((n_in, n_dp, per, wide), BF16),
            pltpu.VMEM((n_in, n_dp, per, wide), BF16),
            pltpu.VMEM((n_out, 2, n_dp, per // 2, wide), BF16),
            pltpu.VMEM((2, n_dp, per // 2, depth), F32),
            pltpu.VMEM((2, n_dp, n_mp // 4, rows, depth), BF16),
            pltpu.VMEM((2, n_dp, n_mp // 4, rows, depth), BF16),
            pltpu.VMEM((2, n_dp, n_mp // 4, rows, depth), BF16),
            pltpu.VMEM((n_dev // 2, rows, depth), BF16),
            dma((3,)), dma((n_in // GROUP,)), dma((n_in // GROUP,)), dma, dma((n_dev // 2,)),
            dma, dma, dma, dma((n_in, 3)), dma, dma((n_out * 6,)), dma, dma((2, n_dp)), dma, dma,
        ],
        compiler_params=pltpu.CompilerParams(
            collective_id=0, has_side_effects=True, vmem_limit_bytes=60 * 1024 * 1024
        ),
        name="encoder_block",
    )(
        tokens, norm_gain.reshape(1, -1), bias_inner.reshape(1, -1), temper,
        w_query, w_key, w_value, w_inner, w_attn_out, w_outer,
    )


def solution(mesh):
    return jax.shard_map(
        functools.partial(per_device, mesh.shape["dp"], mesh.shape["mp"]),
        mesh=mesh,
        in_specs=(
            P(("dp", "mp"), None),
            P(),
            P("dp", "mp"),
            P("dp", "mp"),
            P("dp", "mp"),
            P("dp", "mp"),
            P("mp"),
            P("mp", "dp"),
            P("mp", "dp"),
            P("mp"),
        ),
        out_specs=P(("dp", "mp"), None),
        check_vma=False,
    )
```

time: 47 us -> 43.3 us (0.921)
  Pallas kernels: 45.4 us -> 42.5 us
  local copies, waits for them, and re-layouts: 1.44 us -> 0.62 us
    pallas_call x1, Pallas kernels: 45.4 us -> 42.5 us  [per_device(): pl.pallas_call(functools.partial(block_kernel, n_dp, n_mp), out_shape=plt...]
    unnamed x1, local copies, waits for them, and re-layouts: 1.44 us -> 0.62 us
where the time goes in v1:
time: 43.3 us; the launch traced here: 43.1 us
  Pallas kernels  42.5 us (98%)
  local copies, waits for them, and re-layouts  0.62 us (1%)
    pallas_call x1, Pallas kernels, per_device(): pl.pallas_call(functools.partial(block_kernel, n_dp, n_mp), out_shape=plt...  42.5 us

profile of v1, /device:TPU:0, one launch (start us, length us, event | category | flops | bytes accessed | tf_op | source)
XLA Modules:
  0.0 43.1 jit_solution(2790382605725484217)
XLA Ops:
  0.0 42.5 %encoder_block.1 = bf16[4,6144]{1,0:T(4,128)(2,1)S(1)} custom-call(bf16[4,6144]{1,0:T(4,128)(2,1)} %tokens.1, f32[1,6144]{1,0:T(1,128)} %bitcast.2, f32[1,3072]{1,0:T(1,128)} %bitcast.3, f32[4]{0:T(128)} %temper.1, bf16[1536,512]{1,0:T(8,128)(2,1)} %w_query.1, bf16[1536,512]{1,0:T(8,128)(2,1)} %w_key.1, bf16[1536,512]{1,0:T(8,128)(2,1)} %w_value.1, ...), custom_call_target="tpu_custom_call" | custom-call | tf_op jit(solution)/shard_map/encoder_block/pallas_call | solution.py:361
  42.5 0.6 %copy.12 = bf16[4,6144]{1,0:T(4,128)(2,1)} copy(bf16[4,6144]{1,0:T(4,128)(2,1)S(1)} %encoder_block.1) | data formatting | bytes 98304

commit v2 on v1

v2 whole, which is shorter than its diff:
```python
import functools
import math

import jax
import jax.numpy as jnp
from jax import lax
from jax.experimental import pallas as pl
from jax.experimental.pallas import tpu as pltpu
from jax.sharding import PartitionSpec as P

HEAD = 128
GROUP = 3
MESH = pl.DeviceIdType.MESH
F32, BF16 = jnp.float32, jnp.bfloat16


def normalize(values):
    center = values - jnp.mean(values, axis=-1, keepdims=True)
    spread = jnp.mean(center * center, axis=-1, keepdims=True)
    return center * lax.rsqrt(spread + 1e-06)


def wait_bytes(ref, sem):
    pltpu.make_async_copy(ref, ref, sem).wait()


def block_kernel(
    n_dp, n_mp,
    tokens, gain, bias, temper, w_query, w_key, w_value, w_inner, w_attn, w_outer,
    out,
    tok, gain_v, bias_v, temper_v, w_in, w_out, nsend, nrecv, stage, x, psend, precv, ag, acc,
    xsend, xrecv, dsend, drecv,
    in_sem, win_sem, wout_sem, a_send, a_recv, f_send, f_recv, p_send, p_recv, g_send, g_recv,
    x_send, x_recv, d_send, d_recv,
):
    rows = tok.shape[0]
    n_in, depth, wide = w_in.shape
    n_out = w_out.shape[0]
    rows_half = psend.shape[2]
    per = 2 * rows_half
    n_group = n_in // GROUP
    i, j = lax.axis_index("dp"), lax.axis_index("mp")
    me = i * n_mp + j
    n_chip = n_mp // 2
    n_lane = n_dp * n_chip
    core, chip = lax.rem(j, 2), j // 2
    sibling = (i, j + 1 - 2 * core)
    lane = i * n_chip + chip
    square = n_dp == 4
    n_half = n_chip // 2
    spot = lax.rem(chip, n_half)
    halves = (chip // n_half, 1 - chip // n_half)

    inputs = [
        pltpu.make_async_copy(tokens, tok, in_sem.at[0]),
        pltpu.make_async_copy(gain, gain_v, in_sem.at[1]),
        pltpu.make_async_copy(bias, bias_v, in_sem.at[2]),
        pltpu.make_async_copy(temper, temper_v, in_sem.at[3]),
    ]
    for copy in inputs:
        copy.start()

    barrier = pltpu.get_barrier_semaphore()
    if square:
        beside, across = i + 1 - 2 * lax.rem(i, 2), lax.rem(i + 2, n_dp)
        columns = [i, beside, across, 3 - i]
    else:
        columns = [lax.rem(i + a, n_dp) for a in range(n_dp)]
    chips = [lax.rem(chip + b, n_chip) for b in range(n_chip)]
    for a in range(n_dp):
        for b in range(n_chip):
            if a or b:
                pl.semaphore_signal(
                    barrier, inc=1, device_id=(columns[a], 2 * chips[b] + core),
                    device_id_type=MESH,
                )
    pl.semaphore_signal(barrier, inc=1, device_id=sibling, device_id_type=MESH)

    for copy in inputs:
        copy.wait()
    normed = (normalize(tok[...].astype(F32)) * gain_v[...]).astype(BF16)
    for p in range(n_dp):
        nsend[p] = normed[:, p * depth : (p + 1) * depth]
    nrecv[me] = nsend[i]
    pl.semaphore_wait(barrier, n_lane)

    def pass_on(far, source):
        pltpu.make_async_remote_copy(
            src_ref=nrecv.at[source], dst_ref=nrecv.at[source],
            send_sem=f_send, recv_sem=f_recv.at[far],
            device_id=sibling, device_id_type=MESH,
        ).start()

    def outer_first(b):
        return b + (1 - halves[0]) * (n_half - 1 - 2 * b)

    for far in range(2):
        for b in range(n_half):
            b = b if far else n_half - 1 - b
            spot_to = outer_first(b) if far else lax.rem(spot + b, n_half)
            for a in reversed(range(n_dp)):
                if far or a or b:
                    pltpu.make_async_remote_copy(
                        src_ref=nsend.at[columns[a]], dst_ref=nrecv.at[me],
                        send_sem=a_send, recv_sem=a_recv.at[n_half + spot if far else b],
                        device_id=(columns[a], 2 * (halves[far] * n_half + spot_to) + core),
                        device_id_type=MESH,
                    ).start()
    pass_on(0, me)
    for c, w in enumerate((w_query, w_key, w_value)):
        pltpu.make_async_copy(w, w_in.at[c], win_sem.at[0]).start()
    for c in range(3, n_in):
        pltpu.make_async_copy(
            w_inner.at[:, pl.ds((c - 3) * wide, wide)], w_in.at[c], win_sem.at[c // GROUP]
        ).start()
    pltpu.make_async_copy(w_attn, w_out.at[0], wout_sem.at[0]).start()
    for c in range(1, n_out):
        pltpu.make_async_copy(
            w_outer.at[pl.ds((c - 1) * wide, wide), :], w_out.at[c],
            wout_sem.at[(c - 1) // GROUP + 1],
        ).start()

    def forward(far):
        for step in range(n_half):
            b = far * n_half + step
            spot_from = step if far else lax.rem(spot + n_half - step, n_half)
            source = 2 * (halves[far] * n_half + spot_from) + core
            first = 0 if b else 1
            wait_bytes(nrecv.at[pl.ds(0, n_dp - first)], a_recv.at[b])
            for a in range(first, n_dp):
                pass_on(far, columns[a] * n_mp + source)

    def gather(far):
        wait_bytes(nrecv.at[pl.ds(0, n_lane // 2)], f_recv.at[far])
        for p in range(n_dp):
            for k in range(n_chip):
                s = p * n_chip + k
                source = p * n_mp + halves[far] * n_chip + k
                stage[s * rows : (s + 1) * rows, :] = nrecv[source].astype(F32)
        x[far] = stage[...].astype(BF16)

    forward(0)
    gather(0)

    def around(t):
        turn = lax.rem(t + core, 2)
        return beside + turn * (across - beside), across + turn * (beside - across)

    def send(source, target, send_sem, recv_sem, p):
        pltpu.make_async_remote_copy(
            src_ref=source, dst_ref=target, send_sem=send_sem, recv_sem=recv_sem,
            device_id=(p, j), device_id_type=MESH,
        ).start()

    def project(far, g, early, fetch):
        if fetch:
            wait_bytes(w_in.at[pl.ds(g * GROUP, GROUP)], win_sem.at[g])
        def multiply(r):
            c = g * GROUP + r
            part = jnp.dot(x[far], w_in[c], preferred_element_type=F32).astype(BF16)
            psend[far * n_in + c] = part.reshape(n_dp, rows_half, wide)

        def scatter(r):
            t = far * n_in + g * GROUP + r
            lamp = p_recv.at[2 * (far * n_group + g)]
            if square:
                nearby, _ = around(t)
                send(psend.at[t, 3 - i], precv.at[t, 1], p_send, lamp, nearby)
                send(psend.at[t, nearby], precv.at[t, 0], p_send, lamp, nearby)
            else:
                precv[t, i] = psend[t, i]
                for d in range(1, n_dp):
                    send(psend.at[t, columns[d]], precv.at[t, i], p_send, lamp, columns[d])

        for r in range(GROUP):
            multiply(r)
            if r < early:
                scatter(r)
        for r in range(early, GROUP):
            scatter(r)

    def add_and_send(far, g):
        if not square:
            return
        u = far * n_group + g
        start = far * n_in + g * GROUP
        wait_bytes(precv.at[pl.ds(start, GROUP), pl.ds(0, 2)], p_recv.at[2 * u])
        seconds = [around(start + r)[1] for r in range(GROUP)]
        for r in range(GROUP):
            t = start + r
            precv[t, 3] = (psend[t, seconds[r]].astype(F32) + precv[t, 1].astype(F32)).astype(BF16)
        for r in range(GROUP):
            t = start + r
            send(precv.at[t, 3], precv.at[t, 2], p_send, p_recv.at[2 * u + 1], seconds[r])

    def arrived(far, g):
        u = far * n_group + g
        if square:
            wait_bytes(precv.at[pl.ds(far * n_in + g * GROUP, GROUP), 2], p_recv.at[2 * u + 1])
        else:
            start = far * n_in + g * GROUP
            wait_bytes(precv.at[pl.ds(start, GROUP), pl.ds(0, n_dp - 1)], p_recv.at[2 * u])

    def reduced(far, c):
        t = far * n_in + c
        if square:
            total = psend[t, i].astype(F32) + precv[t, 0].astype(F32)
            return total + precv[t, 2].astype(F32)
        total = precv[t, 0].astype(F32)
        for p in range(1, n_dp):
            total = total + precv[t, p].astype(F32)
        return total

    def members(g):
        return [0] if g == 0 else [(g - 1) * GROUP + 1 + r for r in range(GROUP)]

    def lamp_of(far, g, step):
        return g_recv.at[2 * (far * n_group + g) + min(step, 1)]

    def share(far, g):
        for h in members(g):
            own = ag.at[h, far, i]
            if square:
                first, second = around(h)
                send(own, own, g_send, lamp_of(far, g, 0), second)
                send(own, own, g_send, lamp_of(far, g, 1), first)
            else:
                for d in range(1, n_dp):
                    send(own, own, g_send, lamp_of(far, g, 0), columns[d])

    def hand_over(far, g):
        if not square:
            return
        hs = members(g)
        wait_bytes(ag.at[pl.ds(hs[0], len(hs)), far, 0], lamp_of(far, g, 0))
        for h in hs:
            first, second = around(h)
            block = ag.at[h, far, second]
            send(block, block, g_send, lamp_of(far, g, 2), first)

    def attend():
        for far in range(2):
            arrived(far, 0)
        query, key, value = (
            jnp.concatenate([reduced(0, c), reduced(1, c)], axis=0).astype(BF16) for c in range(3)
        )
        heads = range(wide // HEAD)
        cols = [slice(h * HEAD, (h + 1) * HEAD) for h in heads]
        tall = [t[:, cols[h]].astype(F32) for t in (query, key) for h in heads]
        tall = normalize(jnp.concatenate(tall, axis=0)).astype(BF16)
        pairs = [
            (tall[h * per : (h + 1) * per], tall[(len(heads) + h) * per : (len(heads) + h + 1) * per])
            for h in heads
        ]
        scores = jnp.concatenate([
            lax.dot_general(q, k, (((1,), (1,)), ((), ())), preferred_element_type=F32)
            * (temper_v[:, h : h + 1] * (1.0 / math.sqrt(HEAD)))
            for h, (q, k) in zip(heads, pairs)
        ], axis=0)
        weight = jnp.exp(scores - jnp.max(scores, axis=-1, keepdims=True))
        probs = (weight / jnp.sum(weight, axis=-1, keepdims=True)).astype(BF16)
        mixed = [
            jnp.dot(
                probs[h * per : (h + 1) * per], value[:, cols[h]], preferred_element_type=F32
            ).astype(BF16)
            for h in heads
        ]
        mixed = jnp.concatenate(mixed, axis=1)
        for far in range(2):
            ag[0, far, i] = mixed[far * rows_half : (far + 1) * rows_half]

    def activate(far, g):
        arrived(far, g)
        hs = members(g)
        values = []
        for h in hs:
            at = (h - 1) * wide
            inner = reduced(far, h + 2) + bias_v[:, at : at + wide]
            activ = 0.5 * inner * (1.0 + lax.erf(inner * math.sqrt(0.5)))
            values.append(activ.astype(BF16))
        for h, value in zip(hs, values):
            ag[h, far, i] = value

    def project_out(far, g, opened, fetch):
        hs = members(g)
        if fetch:
            wait_bytes(w_out.at[pl.ds(0, len(hs))], wout_sem.at[g])
        if square:
            both = ag.at[pl.ds(hs[0], len(hs)), far, pl.ds(0, 2)]
            wait_bytes(both, lamp_of(far, g, 1))
        else:
            wait_bytes(ag.at[pl.ds(hs[0], len(hs)), far, pl.ds(0, n_dp - 1)], lamp_of(far, g, 0))
        total = acc[far].reshape(-1, depth) if opened else None
        left = [ag[h, far].reshape(-1, wide) for h in hs]
        left = jnp.concatenate(left, axis=1) if len(hs) > 1 else left[0]
        right = w_out[hs[0] : hs[0] + len(hs)].reshape(-1, depth)
        product = jnp.dot(left, right, preferred_element_type=F32)
        total = product if total is None else total + product
        acc[far] = total.reshape(acc.shape[1:])

    def sorted_rows(half, p, q):
        tile = acc[half, p, 2 * rows * q : 2 * rows * (q + 1), :]
        low, high = tile[:rows], tile[rows:]
        return jnp.where(core == 0, low, high), jnp.where(core == 0, high, low)

    def swap(half):
        for k in range(n_dp):
            p = columns[n_dp - 1 - k]
            for q in range(n_half):
                xsend[half, p, q] = sorted_rows(half, p, q)[1].astype(BF16)
            pltpu.make_async_remote_copy(
                src_ref=xsend.at[half, p], dst_ref=xrecv.at[half, p],
                send_sem=x_send, recv_sem=x_recv.at[half],
                device_id=sibling, device_id_type=MESH,
            ).start()

    def deliver(half):
        wait_bytes(xrecv.at[half], x_recv.at[half])
        for k in range(n_dp):
            p = columns[n_dp - 1 - k]
            for q in range(n_half):
                dsend[half, p, q] = (
                    sorted_rows(half, p, q)[0] + xrecv[half, p, q].astype(F32)
                ).astype(BF16)
            for b in list(range(1, n_half)) + [0]:
                if half or b or k < n_dp - 1:
                    q = outer_first(b) if half else lax.rem(spot + b, n_half)
                    pltpu.make_async_remote_copy(
                        src_ref=dsend.at[half, p, q], dst_ref=drecv.at[lane],
                        send_sem=d_send, recv_sem=d_recv,
                        device_id=(p, 2 * (halves[half] * n_half + q) + core),
                        device_id_type=MESH,
                    ).start()
        if not half:
            drecv[lane] = dsend[0, i, spot]

    project(0, 0, 0, True)
    forward(1)
    project(0, 1, 0, True)
    gather(1)
    project(1, 1, 0, False)
    project(1, 2, 0, True)
    project(1, 0, 0, False)
    add_and_send(0, 0)
    add_and_send(0, 1)
    project(0, 2, 0, False)
    add_and_send(1, 1)
    add_and_send(1, 2)
    add_and_send(1, 0)
    add_and_send(0, 2)
    activate(0, 1)
    share(0, 1)
    activate(1, 1)
    share(1, 1)
    activate(1, 2)
    share(1, 2)
    attend()
    share(1, 0)
    share(0, 0)
    hand_over(0, 1)
    hand_over(1, 1)
    hand_over(1, 2)
    hand_over(1, 0)
    hand_over(0, 0)
    activate(0, 2)
    share(0, 2)
    project_out(0, 1, False, True)
    project_out(1, 1, False, False)
    project_out(1, 2, True, True)
    project_out(1, 0, True, True)
    swap(1)
    hand_over(0, 2)
    deliver(1)
    project_out(0, 0, True, False)
    project_out(0, 2, True, False)
    swap(0)
    deliver(0)
    wait_bytes(drecv.at[pl.ds(0, n_lane - 1)], d_recv)
    for p in range(n_dp):
        total = drecv[p * n_chip].astype(F32)
        for q in range(1, n_chip):
            total = total + drecv[p * n_chip + q].astype(F32)
        cols = slice(p * depth, (p + 1) * depth)
        out[:, cols] = (tok[:, cols].astype(F32) + total).astype(BF16)

    wait_bytes(nrecv.at[pl.ds(0, n_lane - 1)], a_send)
    wait_bytes(nrecv.at[pl.ds(0, n_lane)], f_send)
    wait_bytes(precv.at[:, pl.ds(0, n_dp - 1)], p_send)
    wait_bytes(ag.at[:, :, pl.ds(0, n_dp - 1)], g_send)
    wait_bytes(xrecv, x_send)
    wait_bytes(drecv.at[pl.ds(0, n_lane - 1)], d_send)


def per_device(
    n_dp, n_mp,
    tokens, norm_gain, w_query, w_key, w_value, w_inner, bias_inner, w_attn_out, w_outer, temper
):
    rows, width = tokens.shape
    depth, wide = w_query.shape
    hidden = w_inner.shape[1]
    n_dev, per = n_dp * n_mp, n_mp * rows
    n_in, n_out = 3 + hidden // wide, 1 + hidden // wide
    vmem = pl.BlockSpec(memory_space=pltpu.VMEM)
    hbm = pl.BlockSpec(memory_space=pl.ANY)
    dma = pltpu.SemaphoreType.DMA
    return pl.pallas_call(
        functools.partial(block_kernel, n_dp, n_mp),
        out_shape=pltpu.VMEM((rows, width), BF16),
        in_specs=[hbm] * 10,
        out_specs=vmem,
        scratch_shapes=[
            pltpu.VMEM((rows, width), BF16),
            pltpu.VMEM((1, width), F32),
            pltpu.VMEM((1, hidden), F32),
            pltpu.VMEM((1, wide // HEAD), F32),
            pltpu.VMEM((n_in, depth, wide), BF16),
            pltpu.VMEM((n_out, wide, depth), BF16),
            pltpu.VMEM((n_dp, rows, depth), BF16),
            pltpu.VMEM((n_dev, rows, depth), BF16),
            pltpu.VMEM((n_dev * rows // 2, depth), F32),
            pltpu.VMEM((2, n_dev * rows // 2, depth), BF16),
            pltpu.VMEM((2 * n_in, n_dp, per // 2, wide), BF16),
            pltpu.VMEM((2 * n_in, n_dp, per // 2, wide), BF16),
            pltpu.VMEM((n_out, 2, n_dp, per // 2, wide), BF16),
            pltpu.VMEM((2, n_dp, per // 2, depth), F32),
            pltpu.VMEM((2, n_dp, n_mp // 4, rows, depth), BF16),
            pltpu.VMEM((2, n_dp, n_mp // 4, rows, depth), BF16),
            pltpu.VMEM((2, n_dp, n_mp // 4, rows, depth), BF16),
            pltpu.VMEM((n_dev // 2, rows, depth), BF16),
            dma((4,)), dma((n_in // GROUP,)), dma((n_in // GROUP,)), dma, dma((n_mp // 2,)),
            dma, dma((2,)), dma, dma((4 * (n_in // GROUP),)), dma, dma((4 * (n_in // GROUP),)),
            dma, dma((2,)), dma, dma,
        ],
        compiler_params=pltpu.CompilerParams(
            collective_id=0, has_side_effects=True, vmem_limit_bytes=60 * 1024 * 1024
        ),
        name="encoder_block",
    )(
        tokens, norm_gain.reshape(1, -1), bias_inner.reshape(1, -1), temper.reshape(1, -1),
        w_query, w_key, w_value, w_inner, w_attn_out, w_outer,
    )


def solution(mesh):
    return jax.shard_map(
        functools.partial(per_device, mesh.shape["dp"], mesh.shape["mp"]),
        mesh=mesh,
        in_specs=(
            P(("dp", "mp"), None),
            P(),
            P("dp", "mp"),
            P("dp", "mp"),
            P("dp", "mp"),
            P("dp", "mp"),
            P("mp"),
            P("mp", "dp"),
            P("mp", "dp"),
            P("mp"),
        ),
        out_specs=P(("dp", "mp"), None),
        check_vma=False,
    )
```

time: 43.3 us -> 41.8 us (0.965)
  Pallas kernels: 42.5 us -> 41 us
    pallas_call x1, Pallas kernels: 42.5 us -> 41 us  [per_device(): pl.pallas_call(functools.partial(block_kernel, n_dp, n_mp), out_shape=plt...]
where the time goes in v2:
time: 41.8 us; the launch traced here: 41.7 us
  Pallas kernels  41 us (98%)
  local copies, waits for them, and re-layouts  0.62 us (1%)
    pallas_call x1, Pallas kernels, per_device(): pl.pallas_call(functools.partial(block_kernel, n_dp, n_mp), out_shape=plt...  41 us

profile of v2, /device:TPU:0, one launch (start us, length us, event | category | flops | bytes accessed | tf_op | source)
XLA Modules:
  0.0 41.7 jit_solution(17508444802000879404)
XLA Ops:
  0.0 41.0 %encoder_block.1 = bf16[4,6144]{1,0:T(4,128)(2,1)S(1)} custom-call(bf16[4,6144]{1,0:T(4,128)(2,1)} %tokens.1, f32[1,6144]{1,0:T(1,128)} %bitcast.3, f32[1,3072]{1,0:T(1,128)} %bitcast.4, f32[1,4]{1,0:T(1,128)} %bitcast.5, bf16[1536,512]{1,0:T(8,128)(2,1)} %w_query.1, bf16[1536,512]{1,0:T(8,128)(2,1)} %w_key.1, bf16[1536,512]{1,0:T(8,128)(2,1)} %w_value.1, ...), custom_call_target="tpu_custom_call" | custom-call | tf_op jit(solution)/shard_map/encoder_block/pallas_call | solution.py:406
  41.0 0.6 %copy.12 = bf16[4,6144]{1,0:T(4,128)(2,1)} copy(bf16[4,6144]{1,0:T(4,128)(2,1)S(1)} %encoder_block.1) | data formatting | bytes 98304

commit v3 on v2

--- a/solution.py
+++ b/solution.py
@@ -226,7 +226,7 @@
                 send(own, own, g_send, lamp_of(far, g, 1), first)
             else:
                 for d in range(1, n_dp):
-                    send(own, own, g_send, lamp_of(far, g, 0), columns[d])
+                    send(own, own, g_send, lamp_of(far, g, 1), columns[d])
 
     def hand_over(far, g):
         if not square:
@@ -285,11 +285,8 @@
         hs = members(g)
         if fetch:
             wait_bytes(w_out.at[pl.ds(0, len(hs))], wout_sem.at[g])
-        if square:
-            both = ag.at[pl.ds(hs[0], len(hs)), far, pl.ds(0, 2)]
-            wait_bytes(both, lamp_of(far, g, 1))
-        else:
-            wait_bytes(ag.at[pl.ds(hs[0], len(hs)), far, pl.ds(0, n_dp - 1)], lamp_of(far, g, 0))
+        others = 2 if square else n_dp - 1
+        wait_bytes(ag.at[pl.ds(hs[0], len(hs)), far, pl.ds(0, others)], lamp_of(far, g, 1))
         total = acc[far].reshape(-1, depth) if opened else None
         left = [ag[h, far].reshape(-1, wide) for h in hs]
         left = jnp.concatenate(left, axis=1) if len(hs) > 1 else left[0]
@@ -343,13 +340,13 @@
     project(1, 0, 0, False)
     add_and_send(0, 0)
     add_and_send(0, 1)
+    add_and_send(1, 1)
     project(0, 2, 0, False)
-    add_and_send(1, 1)
     add_and_send(1, 2)
     add_and_send(1, 0)
-    add_and_send(0, 2)
     activate(0, 1)
     share(0, 1)
+    add_and_send(0, 2)
     activate(1, 1)
     share(1, 1)
     activate(1, 2)

time: 41.8 us -> 41.4 us (level)
    pallas_call x1, Pallas kernels: 41 us -> 40.6 us  [per_device(): pl.pallas_call(functools.partial(block_kernel, n_dp, n_mp), out_shape=plt...]
where the time goes in v3:
time: 41.4 us; the launch traced here: 41.2 us
  Pallas kernels  40.6 us (98%)
  local copies, waits for them, and re-layouts  0.62 us (1%)
    pallas_call x1, Pallas kernels, per_device(): pl.pallas_call(functools.partial(block_kernel, n_dp, n_mp), out_shape=plt...  40.6 us

profile of v3, /device:TPU:0, one launch (start us, length us, event | category | flops | bytes accessed | tf_op | source)
XLA Modules:
  0.0 41.2 jit_solution(1476394484549604893)
XLA Ops:
  0.0 40.6 %encoder_block.1 = bf16[4,6144]{1,0:T(4,128)(2,1)S(1)} custom-call(bf16[4,6144]{1,0:T(4,128)(2,1)} %tokens.1, f32[1,6144]{1,0:T(1,128)} %bitcast.3, f32[1,3072]{1,0:T(1,128)} %bitcast.4, f32[1,4]{1,0:T(1,128)} %bitcast.5, bf16[1536,512]{1,0:T(8,128)(2,1)} %w_query.1, bf16[1536,512]{1,0:T(8,128)(2,1)} %w_key.1, bf16[1536,512]{1,0:T(8,128)(2,1)} %w_value.1, ...), custom_call_target="tpu_custom_call" | custom-call | tf_op jit(solution)/shard_map/encoder_block/pallas_call | solution.py:403
  40.6 0.6 %copy.12 = bf16[4,6144]{1,0:T(4,128)(2,1)} copy(bf16[4,6144]{1,0:T(4,128)(2,1)S(1)} %encoder_block.1) | data formatting | bytes 98304
